TPU v7x, 256 devices: a whole 4x4x8 slice. The times are simulated.
256 devices in a mesh: blk: 4 (over z_lo), pts: 64 (over y, z_hi, x, core).
Axes of the slice: x: 4, y: 4, z: 8 (z_hi: 2, z_lo: 4; z = z_hi * 4 + z_lo), core: 2. Of those that a mesh axis runs over, the one named last changes fastest.
Arguments:
- signal: bfloat16 [67584, 16384], P('blk', 'pts'), may hold values from -6 to 6
- offsets: int32 [128], P('blk'), may hold values from 0 to 15872
- kept: int32 [128], replicated, may hold values from 0 to 512
- weights: float32 [16384], P('pts'), may hold values from 0.2 to 5
Outputs:
- gram: float32 [128, 2, 128, 128], P('pts', None, 'blk')
Inputs may be any that keep to these rules, and one draw needn't show every extreme that they name: `kept`: indices may repeat.
All inputs are finite; a program needn't handle non-finite values.
Results may differ from a plain program's by a relative error of at most 0.0022.
Values may be sent and summed in bfloat16 or wider, within the bound.
A program may use at most 128 MiB of HBM per device.

v0:
```python
import math

import jax
import jax.numpy as jnp
from jax import lax
from jax.sharding import PartitionSpec as P

NFFT = 1024


def spectral_table(kept, length):
    times = jnp.arange(length, dtype=jnp.int32)
    window = 0.5 - 0.5 * jnp.cos(times.astype(jnp.float32) * (2.0 * math.pi / length))
    norm = 1.0 / jnp.sqrt(jnp.sum(window * window))
    phase_index = times[:, None] * kept[None, :] % length
    phase = phase_index.astype(jnp.float32) * (2.0 * math.pi / length)
    cosine = (norm * window)[:, None] * jnp.cos(phase)
    sine = -(norm * window)[:, None] * jnp.sin(phase)
    return jnp.concatenate([cosine, sine], axis=1).astype(jnp.bfloat16)


def gram_terms(owned, piece):
    own_re = owned[:, 0]
    own_im = owned[:, 1]
    far_re = piece[:, 0]
    far_im = piece[:, 1]
    gram_re = jnp.einsum("bfp,nfp->fbn", own_re, far_re, preferred_element_type=jnp.float32)
    gram_re = gram_re + jnp.einsum(
        "bfp,nfp->fbn", own_im, far_im, preferred_element_type=jnp.float32
    )
    gram_im = jnp.einsum("bfp,nfp->fbn", own_re, far_im, preferred_element_type=jnp.float32)
    gram_im = gram_im - jnp.einsum(
        "bfp,nfp->fbn", own_im, far_re, preferred_element_type=jnp.float32
    )
    return jnp.stack([gram_re, gram_im], axis=1)


def on_device(signal, offsets, kept, weights):
    blocks_here = offsets.shape[0]
    points_here = signal.shape[1]
    freq_all = kept.shape[0]
    total_points = points_here * lax.axis_size("pts")
    table = spectral_table(kept, NFFT)

    def take_block(start):
        return lax.dynamic_slice(signal, (start, jnp.int32(0)), (NFFT, points_here))

    stacked = jax.vmap(take_block)(offsets)
    values = jnp.einsum("tk,btp->bkp", table, stacked, preferred_element_type=jnp.float32)
    scale = jnp.sqrt(weights / total_points)
    spectra = (
        (values * scale[None, None, :])
        .astype(jnp.bfloat16)
        .reshape(blocks_here, 2, freq_all, points_here)
    )
    moved = lax.all_to_all(spectra, "pts", split_axis=2, concat_axis=3, tiled=True)
    return gram_terms(moved, lax.all_gather(moved, "blk", axis=0, tiled=True))


def solution(mesh):
    placed = (P("blk", "pts"), P("blk"), P(), P("pts"))
    return jax.shard_map(
        on_device,
        mesh=mesh,
        in_specs=placed,
        out_specs=P("pts", None, "blk", None),
        check_vma=False,
    )
```

profile of v0, /device:TPU:1, one launch (start us, length us, event | category | flops | bytes accessed | tf_op | source)
XLA Modules:
  0.0 571.0 jit_solution(12233491624750584674)
XLA Ops:
  6.5 0.7 multiply_reduce_fusion
  7.3 0.7 multiply_sqrt_fusion
  7.9 0.7 fusion.18
  8.6 99.7 %while.1 = (s32[]{:T(128)}, bf16[16896,256]{1,0:T(8,128)(2,1)}, s32[32,2]{0,1:T(2,128)S(1)}, bf16[32,1024,256]{2,1,0:T(8,128)(2,1)}, s32[]{:T(128)}) while((s32[]{:T(128)}, bf16[16896,256]{1,0:T(8,128)(2,1)}, s32[32,2]{0,1:T(2,128)S(1)}, bf16[32,1024,256]{2,1,0:T(8,128)(2,1)}, s32[]{:T(128)}) %tuple.18), condition=%wide.while_cond, body=%wide.while_body.sunk | while | flops 2 | bytes 1049189 | solution.py:46
  9.2 2.5 bitcast_dynamic-update-slice_fusion.2
  12.3 2.5 bitcast_dynamic-update-slice_fusion.2
  15.4 2.5 bitcast_dynamic-update-slice_fusion.2
  18.0 0.5 slice.60
  18.5 2.5 bitcast_dynamic-update-slice_fusion.2
  21.6 2.5 bitcast_dynamic-update-slice_fusion.2
  24.2 0.5 slice.60
  24.7 2.5 bitcast_dynamic-update-slice_fusion.2
  27.9 2.5 bitcast_dynamic-update-slice_fusion.2
  30.5 0.5 slice.60
  31.0 2.5 bitcast_dynamic-update-slice_fusion.2
  33.6 0.5 slice.60
  34.1 2.5 bitcast_dynamic-update-slice_fusion.2
  37.2 2.5 bitcast_dynamic-update-slice_fusion.2
  39.8 0.5 slice.60
  40.3 2.5 bitcast_dynamic-update-slice_fusion.2
  43.0 0.5 slice.60
  43.5 2.5 bitcast_dynamic-update-slice_fusion.2
  46.1 0.5 slice.60
  46.6 2.5 bitcast_dynamic-update-slice_fusion.2
  49.2 0.5 slice.60
  49.7 2.5 bitcast_dynamic-update-slice_fusion.2
  52.3 0.5 slice.60
  52.8 2.5 bitcast_dynamic-update-slice_fusion.2
  55.4 0.5 slice.60
  55.9 2.6 bitcast_dynamic-update-slice_fusion.2
  58.5 0.5 slice.60
  59.1 2.6 bitcast_dynamic-update-slice_fusion.2
  62.2 2.6 bitcast_dynamic-update-slice_fusion.2
  64.8 0.5 slice.60
  65.4 2.5 bitcast_dynamic-update-slice_fusion.2
  67.9 0.5 slice.60
  68.5 2.5 bitcast_dynamic-update-slice_fusion.2
  71.0 0.5 slice.60
  71.5 2.6 bitcast_dynamic-update-slice_fusion.2
  74.2 0.5 slice.60
  74.7 2.5 bitcast_dynamic-update-slice_fusion.2
  77.8 2.5 bitcast_dynamic-update-slice_fusion.2
  80.4 0.5 slice.60
  80.9 2.5 bitcast_dynamic-update-slice_fusion.2
  84.0 2.6 bitcast_dynamic-update-slice_fusion.2
  87.1 2.5 bitcast_dynamic-update-slice_fusion.2
  90.3 2.5 bitcast_dynamic-update-slice_fusion.2
  93.4 2.5 bitcast_dynamic-update-slice_fusion.2
  96.5 2.5 bitcast_dynamic-update-slice_fusion.2
  99.6 2.5 bitcast_dynamic-update-slice_fusion.2
  102.7 2.5 bitcast_dynamic-update-slice_fusion.2
  105.8 2.5 bitcast_dynamic-update-slice_fusion.2
  109.1 3.1 multiply_convert_fusion.2
  112.3 12.1 %multiply_convert_fusion = bf16[32,256,256]{1,2,0:T(8,128)(2,1)} fusion(f32[256]{0:T(256)S(1)} %multiply_sqrt_fusion, bf16[32,1024,256]{2,1,0:T(8,128)(2,1)} %get-tuple-element.12, bf16[1024,128]{0,1:T(8,128)(2,1)S(1)} %get-tuple-element.22, bf16[1024,128]{0,1:T(8,128)(2,1)S(1)} %get-tuple-element.21), kind=kOutput, calls=%fused_computation.4 | convolution fusion | flops 4300210176 | bytes 21496832 | tf_op jit(solution)/shard_map/tk,btp->bkp/dot_general | solution.py:49
  124.4 6.5 %copy.7 = bf16[32,2,128,256]{3,1,0,2:T(2,128)(2,1)S(1)} copy(bf16[32,2,128,256]{3,2,1,0:T(8,128)(2,1)} %bitcast.62) | data formatting | bytes 8388608 | tf_op jit(solution)/shard_map/reshape | solution.py:54
  130.9 115.3 %all_to_all.18 = bf16[32,2,128,256]{3,1,0,2:T(2,128)(2,1)S(1)} all-to-all(bf16[32,2,128,256]{3,1,0,2:T(2,128)(2,1)S(1)} %copy.7), channel_id=1, replica_groups=mesh['blk'=4,'pts'=64] {'pts'}, dimensions={2} | all-to-all | bytes 8388608 | tf_op jit(solution)/shard_map/all_to_all | solution.py:56
  246.2 4.4 copy.11
  250.5 7.4 %all_to_all.16 = bf16[32,2,2,16384]{3,0,2,1:T(8,128)(2,1)} reshape(bf16[32,2,2,64,256]{4,3,0,2,1:T(8,128)(2,1)} %bitcast.61) | data formatting | bytes 8388608 | tf_op jit(solution)/shard_map/all_to_all | solution.py:56
  257.9 285.5 %all-gather.2.cloned.1.call-done = bf16[128,2,2,16384]{3,0,2,1:T(8,128)(2,1)} async-done(((bf16[32,2,2,16384]{3,0,2,1:T(8,128)(2,1)}), bf16[128,2,2,16384]{3,0,2,1:T(8,128)(2,1)}) %all-gather.2.cloned.1.call-update) | async-done | bytes 16777232 | tf_op jit(solution)/shard_map/all_gather | solution.py:57
  543.4 7.1 %fusion = f32[2,32,128]{2,1,0:T(8,128)S(1)} fusion(bf16[128,2,2,16384]{3,0,2,1:T(8,128)(2,1)} %all-gather.2.cloned.1.call-done, bf16[32,2,2,16384]{3,0,2,1:T(8,128)(2,1)} %all_to_all.16), kind=kOutput, calls=%fused_computation.5 | convolution fusion | flops 268435456 | bytes 10518528 | tf_op jit(solution)/shard_map/bfp,nfp->fbn/dot_general | solution.py:32
  550.5 7.0 %fusion.1 = f32[2,32,128]{2,1,0:T(8,128)S(1)} fusion(bf16[128,2,2,16384]{3,0,2,1:T(8,128)(2,1)} %all-gather.2.cloned.1.call-done, bf16[32,2,2,16384]{3,0,2,1:T(8,128)(2,1)S(1)} %copy-done), kind=kOutput, calls=%fused_computation.6 | convolution fusion | flops 268435456 | bytes 10518528 | tf_op jit(solution)/shard_map/bfp,nfp->fbn/dot_general | solution.py:27
  557.6 2.9 fusion.7
  560.5 3.0 fusion.5
  563.5 0.6 copy.9
  (58 shorter events, 10.6 us)
Async XLA Ops:
  6.5 536.9 %all-gather.2.cloned.1.call-start = ((), (), s32[]{:S(2)}) async-start(), calls=%async_computation.1 | async-start | bytes 20971520 | tf_op jit(solution)/shard_map/all_gather | solution.py:57
  543.4 7.1 %copy-start = (bf16[32,2,2,16384]{3,0,2,1:T(8,128)(2,1)S(1)}, bf16[32,2,2,16384]{3,0,2,1:T(8,128)(2,1)}, u32[]{:S(2)}) copy-start(bf16[32,2,2,16384]{3,0,2,1:T(8,128)(2,1)} %all_to_all.16) | copy-start | bytes 12582916
  543.4 14.1 %copy-start.1 = (bf16[128,2,2,16384]{3,0,2,1:T(8,128)(2,1)S(1)}, bf16[128,2,2,16384]{3,0,2,1:T(8,128)(2,1)}, u32[]{:S(2)}) copy-start(bf16[128,2,2,16384]{3,0,2,1:T(8,128)(2,1)} %all-gather.2.cloned.1.call-done) | copy-start | bytes 50331652
Sparse Core Ops, SparseCore 0:
  258.1 285.3 all-gather.1
where the time goes:
time: 573 us; the launch traced here: 571 us
  waiting for transfers between devices  286 us (50%)
  local copies, waits for them, and re-layouts  119 us (21%)
  blocking collectives  115 us (20%)
  matrix products  32 us (6%)
  between operations  14.2 us (2%)
    all_gather x1, waiting for transfers between devices, on_device(): return gram_terms(moved, lax.all_gather(moved, 'blk', axis=0, tiled=True))  285 us
    all_to_all x1, blocking collectives, on_device(): lax.all_to_all(spectra, 'pts', split_axis=2, concat_axis=3, tiled=True)  115 us
    gather x96, local copies, waits for them, and re-layouts  99.7 us
    dot_general x1, matrix products, on_device(): jnp.einsum('tk,btp->bkp', table, stacked, preferred_element_type=jnp.floa...  12.1 us
    all_to_all x2, local copies, waits for them, and re-layouts, on_device(): lax.all_to_all(spectra, 'pts', split_axis=2, concat_axis=3, tiled=True)  11.8 us
  transfers between devices with their start and end apart: 1, of which 1 were waited for; matrix products, arithmetic and copies ran while one was open for 0% of the time, Pallas kernels for 0%

commit v1 on v0

v1 whole, which is shorter than its diff:
```python
import math

import jax
import jax.numpy as jnp
from jax import lax
from jax.experimental import pallas as pl
from jax.experimental.pallas import tpu as pltpu
from jax.sharding import PartitionSpec as P

NFFT = 1024
ALIGN = 16
LONG = NFFT + 128


def spectral_table(kept, length):
    times = jnp.arange(length, dtype=jnp.int32)
    window = 0.5 - 0.5 * jnp.cos(times.astype(jnp.float32) * (2.0 * math.pi / length))
    norm = 1.0 / jnp.sqrt(jnp.sum(window * window))
    phase_index = kept[:, None] * times[None, :] % length
    phase = phase_index.astype(jnp.float32) * (2.0 * math.pi / length)
    cosine = (norm * window)[None, :] * jnp.cos(phase)
    sine = -(norm * window)[None, :] * jnp.sin(phase)
    both = jnp.stack([cosine, sine], axis=1).reshape(2 * kept.shape[0], length)
    return both.astype(jnp.bfloat16)


def spectra_kernel(
    offsets_ref, table_ref, scale_ref, signal_ref, out_ref, held, shifted, wide, sem
):
    rows_in = signal_ref.shape[0]
    blocks = offsets_ref.shape[0]
    rows, points = table_ref.shape[0], signal_ref.shape[1]
    dests = out_ref.shape[0]
    fetch = pltpu.make_async_copy(signal_ref, held.at[pl.ds(0, rows_in)], sem)
    fetch.start()
    held[pl.ds(rows_in, 128)] = jnp.zeros((128, points), jnp.bfloat16)
    padded = jnp.concatenate(
        [table_ref[...], jnp.zeros((rows, LONG - NFFT), jnp.float32)], axis=1
    )
    shifted[0] = padded.astype(jnp.bfloat16)

    def shift(r, carry):
        shifted[r] = pltpu.roll(padded, r, 1).astype(jnp.bfloat16)
        return carry

    lax.fori_loop(1, ALIGN, shift, 0)
    fetch.wait()
    scale = scale_ref[...]

    def one_block(n, carry):
        start = offsets_ref[n]
        base = pl.multiple_of((start // ALIGN) * ALIGN, ALIGN)
        window = held[pl.ds(base, LONG), :]
        values = jnp.dot(
            shifted[start % ALIGN], window, preferred_element_type=jnp.float32
        )
        values = values * scale
        wide[0, n, pl.ds(0, rows), :] = values[:, :128]
        wide[1, n, pl.ds(0, rows), :] = values[:, 128:]
        return carry

    lax.fori_loop(0, blocks, one_block, 0)
    flat = wide.reshape(2, blocks * wide.shape[2], 128)
    half = rows // 2

    def place(step, carry):
        for inner in range(2):
            for h in range(2):
                for c in range(2):
                    for j in range(2):
                        q = step * 2 + inner
                        row = j * half + 2 * q + c
                        picked = flat[h, pl.ds(row, blocks, stride=wide.shape[2]), :]
                        out_ref[(j * 2 + h) * (dests // 4) + q, pl.ds(c * blocks, blocks), :] = (
                            picked.astype(jnp.bfloat16)
                        )
        return carry

    lax.fori_loop(0, dests // 8, place, 0)


def gram_kernel(got_ref, out_ref):
    blks, groups, rows, lanes = got_ref.shape
    per_blk = rows // 2
    together = 8

    def some(step, total):
        pieces = []
        for i in range(together):
            p = step * together + i
            re = got_ref[:, p, :per_blk, :].reshape(blks * per_blk, lanes)
            im = got_ref[:, p, per_blk:, :].reshape(blks * per_blk, lanes)
            pieces.append(jnp.concatenate([re, im], axis=0))
        x = jnp.concatenate(pieces, axis=1)
        return total + lax.dot_general(
            x, x, (((1,), (1,)), ((), ())), preferred_element_type=jnp.float32
        )

    size = 2 * blks * per_blk
    total = lax.fori_loop(
        0, groups // together, some, jnp.zeros((size, size), jnp.float32)
    )
    nb = size // 2
    gram_re = total[:nb, :nb] + total[nb:, nb:]
    gram_im = total[:nb, nb:] - total[nb:, :nb]
    out_ref[:, 0] = gram_re.reshape(blks, per_blk, nb)
    out_ref[:, 1] = gram_im.reshape(blks, per_blk, nb)


def on_device(signal, offsets, kept, weights):
    blocks_here = offsets.shape[0]
    points_here = signal.shape[1]
    freqs = kept.shape[0]
    blks = lax.axis_size("blk")
    groups = lax.axis_size("pts")
    dests = blks * groups
    per_group = freqs // groups
    ordered = kept.reshape(groups, per_group).T.reshape(freqs)
    table = spectral_table(ordered, NFFT).astype(jnp.float32)
    scale = jnp.sqrt(weights / (points_here * groups)).reshape(1, points_here)
    vmem = pl.BlockSpec(memory_space=pltpu.VMEM)
    sent = pl.pallas_call(
        spectra_kernel,
        out_shape=jax.ShapeDtypeStruct((dests, 2 * blocks_here, 128), jnp.bfloat16),
        in_specs=[
            pl.BlockSpec(memory_space=pltpu.SMEM),
            vmem,
            vmem,
            pl.BlockSpec(memory_space=pl.ANY),
        ],
        out_specs=vmem,
        scratch_shapes=[
            pltpu.VMEM((signal.shape[0] + 128, points_here), jnp.bfloat16),
            pltpu.VMEM((ALIGN, 2 * freqs, LONG), jnp.bfloat16),
            pltpu.VMEM((2, blocks_here, 2 * freqs + 8, 128), jnp.float32),
            pltpu.SemaphoreType.DMA,
        ],
        name="spectra",
    )(offsets, table, scale, signal)
    got = lax.all_to_all(sent, ("blk", "pts"), split_axis=0, concat_axis=0, tiled=True)
    gram = pl.pallas_call(
        gram_kernel,
        out_shape=jax.ShapeDtypeStruct(
            (blks, 2, blocks_here, blks * blocks_here), jnp.float32
        ),
        in_specs=[vmem],
        out_specs=vmem,
        name="gram",
    )(got.reshape(blks, groups, 2 * blocks_here, 128))
    parts = lax.all_to_all(gram, "blk", split_axis=0, concat_axis=0, tiled=True)
    return parts[0::2] + parts[1::2]


def solution(mesh):
    placed = (P("blk", "pts"), P("blk"), P(), P("pts"))
    return jax.shard_map(
        on_device,
        mesh=mesh,
        in_specs=placed,
        out_specs=P("pts", None, "blk", None),
        check_vma=False,
    )
```

time: 573 us -> 161 us (0.28)
  waiting for transfers between devices: 286 us -> 0 us
  local copies, waits for them, and re-layouts: 119 us -> 3.45 us
  matrix products: 32 us -> 0 us
  Pallas kernels: 0 us -> 29.6 us
  between operations: 14.2 us -> 0.74 us
  blocking collectives: 115 us -> 121 us
    all_gather x1 -> x0, waiting for transfers between devices: 285 us -> none  [on_device(): return gram_terms(moved, lax.all_gather(moved, 'blk', axis=0, tiled=True))]
    gather x96 -> x0, local copies, waits for them, and re-layouts: 99.7 us -> none
    dot_general x5 -> x0, matrix products: 32 us -> none  [the longest x1 12.1 us: on_device(): jnp.einsum('tk,btp->bkp', table, stacked, preferred_element_type=jnp.floa...]
    pallas_call x0 -> x2, Pallas kernels: none -> 29.6 us  [the longest x1 24 us: on_device(): pl.pallas_call(spectra_kernel, out_shape=jax.ShapeDtypeStruct((dests, 2 *...]
    all_to_all x2 -> x0, local copies, waits for them, and re-layouts: 11.8 us -> none  [on_device(): lax.all_to_all(spectra, 'pts', split_axis=2, concat_axis=3, tiled=True)]
    all_to_all x1 -> x2, blocking collectives: 115 us -> 121 us  [the longest x1 113 us: on_device(): lax.all_to_all(sent, ('blk', 'pts'), split_axis=0, concat_axis=0, tiled=T...]
  transfers between devices with their start and end apart: 1 -> 0, of which waited for: 1 -> 0; matrix products, arithmetic and copies ran while one was open for 0% -> 0% of each run, Pallas kernels for 0% -> 0%
where the time goes in v1:
time: 161 us; the launch traced here: 160 us
  blocking collectives  121 us (75%)
  Pallas kernels  29.6 us (18%)
  other arithmetic  5.11 us (3%)
  local copies, waits for them, and re-layouts  3.45 us (2%)
    all_to_all x1, blocking collectives, on_device(): lax.all_to_all(sent, ('blk', 'pts'), split_axis=0, concat_axis=0, tiled=T...  113 us
    pallas_call x1, Pallas kernels, on_device(): pl.pallas_call(spectra_kernel, out_shape=jax.ShapeDtypeStruct((dests, 2 *...  24 us
    all_to_all x1, blocking collectives, on_device(): parts = lax.all_to_all(gram, 'blk', split_axis=0, concat_axis=0, tiled=True)  8.06 us
    pallas_call x1, Pallas kernels, on_device(): pl.pallas_call(gram_kernel, out_shape=jax.ShapeDtypeStruct((blks, 2, bloc...  5.61 us

profile of v1, /device:TPU:1, one launch (start us, length us, event | category | flops | bytes accessed | tf_op | source)
XLA Modules:
  0.0 160.0 jit_solution(16860583028247442734)
XLA Ops:
  0.0 0.6 multiply_reduce_fusion
  1.3 1.3 multiply_sqrt_fusion
  2.6 0.8 reshape.182
  3.4 0.1 copy.7
  3.5 0.1 mul.125
  3.6 2.5 %multiply_convert_fusion.1 = (bf16[128,1,1024]{2,0,1:T(8,128)(2,1)S(1)}, bf16[128,1,1024]{2,0,1:T(8,128)(2,1)S(1)}) fusion(s32[128]{0:T(128)S(1)} %mul.125, f32[1024]{0:T(1024)S(1)} %get-tuple-element.7, f32[1024]{0:T(1024)S(1)} %get-tuple-element.8), kind=kLoop, calls=%fused_computation.8 | loop fusion | flops 2359296 | bytes 532992 | tf_op jit(solution)/shard_map/convert.1
  6.1 0.1 maximum_convert_fusion
  6.1 0.8 copy.8
  7.0 1.7 %reshape.185.table_ref = f32[256,1024]{1,0:T(8,128)} reshape(f32[128,2,1024]{2,1,0:T(2,128)S(1)} %copy.8) | data formatting | bytes 2097152 | tf_op jit(solution)/shard_map/convert_element_type | solution.py:119
  8.6 24.0 %spectra.1 = bf16[256,64,128]{2,1,0:T(8,128)(2,1)} custom-call(s32[32]{0:T(128)} %offsets_ref.1, f32[256,1024]{1,0:T(8,128)} %reshape.185.table_ref, f32[1,256]{1,0:T(1,128)} %bitcast.5, bf16[16896,256]{1,0:T(8,128)(2,1)} %signal_ref.1), custom_call_target="tpu_custom_call" | custom-call | tf_op jit(solution)/shard_map/spectra/pallas_call | solution.py:122
  32.6 113.1 %all_to_all.10 = bf16[256,64,128]{2,1,0:T(8,128)(2,1)} all-to-all(bf16[256,64,128]{2,1,0:T(8,128)(2,1)} %spectra.1), channel_id=1, replica_groups=mesh['blk'=4,'pts'=64] {'blk','pts'}, dimensions={0} | all-to-all | bytes 8388608 | tf_op jit(solution)/shard_map/all_to_all | solution.py:140
  145.7 5.6 %gram.1 = f32[4,2,32,128]{3,2,1,0:T(8,128)} custom-call(bf16[4,64,64,128]{3,2,1,0:T(8,128)(2,1)} %bitcast.3), custom_call_target="tpu_custom_call" | custom-call | tf_op jit(solution)/shard_map/gram/pallas_call | solution.py:141
  151.3 8.1 %all_to_all.11 = f32[4,2,32,128]{3,2,1,0:T(8,128)S(1)} all-to-all(f32[4,2,32,128]{3,2,1,0:T(8,128)} %gram.1), channel_id=1, replica_groups=mesh['blk'=4,'pts'=64] {'blk'}, dimensions={0} | all-to-all | bytes 262144 | tf_op jit(solution)/shard_map/all_to_all | solution.py:150
  159.4 0.6 slice_add_fusion
  (1 shorter events, 0.0 us)

commit v2 on v0

v2 whole, which is shorter than its diff:
```python
import math

import jax
import jax.numpy as jnp
import numpy as np
from jax import lax
from jax.experimental import pallas as pl
from jax.experimental.pallas import tpu as pltpu
from jax.sharding import PartitionSpec as P

MESH = pl.DeviceIdType.MESH
NFFT = 1024
ALIGN = 16
LONG = NFFT + 128
PITCH = 8


def spectral_table(kept, length):
    times = jnp.arange(length, dtype=jnp.int32)
    window = 0.5 - 0.5 * np.cos(
        np.arange(length, dtype=np.float32) * np.float32(2.0 * math.pi / length)
    )
    window = window.astype(np.float32)
    norm = np.float32(1.0) / np.sqrt(np.sum(window * window, dtype=np.float32))
    gain = (norm * window).astype(np.float32)[None, :]
    phase_index = kept[:, None] * times[None, :] % length
    phase = phase_index.astype(jnp.float32) * (2.0 * math.pi / length)
    cosine = gain * jnp.cos(phase)
    sine = -gain * jnp.sin(phase)
    return cosine.astype(jnp.bfloat16), sine.astype(jnp.bfloat16)


def fused_kernel(
    offsets_ref, cos_ref, sin_ref, scale_ref, signal_ref, out_ref,
    held, padded, shifted, wide, sent, got, total, handed, final,
    load_sem, send_sem, recv_sem, hand_sem, final_sem,
):
    steps_in, _, points = signal_ref.shape
    freqs = cos_ref.shape[0]
    rows = 2 * freqs
    blocks = offsets_ref.shape[0]
    part = wide.shape[1]
    halves = blocks // part

    blk = lax.axis_index("blk")
    pts = lax.axis_index("pts")
    core = lax.rem(pts, 2)
    x = lax.rem(pts // 2, 4)
    zh = lax.rem(pts // 8, 2)
    y = pts // 16

    def device(b, zh_, y_, x_, c_):
        return (b, ((y_ * 2 + zh_) * 4 + x_) * 2 + c_)

    def slot(b, y_, x_, c_):
        return y_ * 32 + (x_ * 2 + c_) * 4 + b

    def peer(dy, inner):
        turn = inner // 4
        way = lax.rem(inner, 4)
        b2 = jnp.bitwise_xor(blk, jnp.where(way == 0, 2, jnp.where(way == 1, 1, jnp.where(way == 2, 3, 0))))
        y2 = lax.rem(y + dy, 4)
        x2 = lax.rem(x + turn // 2, 4)
        c2 = lax.rem(core + turn, 2)
        return b2, y2, x2, c2

    mine = slot(blk, y, x, core)

    fetch = pltpu.make_async_copy(signal_ref, held.at[pl.ds(0, steps_in)], load_sem)
    fetch.start()

    barrier = pltpu.get_barrier_semaphore()

    def greet(i, carry):
        b2, y2, x2, c2 = peer(i // 32, lax.rem(i, 32))

        @pl.when(i != 3)
        def _():
            pl.semaphore_signal(
                barrier, inc=1, device_id=device(b2, zh, y2, x2, c2), device_id_type=MESH
            )

        return carry

    lax.fori_loop(0, 128, greet, 0)

    def greet_far(b2, carry):
        pl.semaphore_signal(
            barrier, inc=1, device_id=device(b2, 1 - zh, y, x, core), device_id_type=MESH
        )
        return carry

    lax.fori_loop(0, 4, greet_far, 0)

    spare = held.shape[0] - steps_in
    held[pl.ds(steps_in, spare)] = jnp.zeros((spare, ALIGN, points), jnp.bfloat16)
    padded[pl.ds(0, freqs), pl.ds(0, NFFT)] = cos_ref[...].astype(jnp.float32)
    padded[pl.ds(freqs, freqs), pl.ds(0, NFFT)] = sin_ref[...].astype(jnp.float32)
    padded[:, pl.ds(NFFT, LONG - NFFT)] = jnp.zeros((rows, LONG - NFFT), jnp.float32)

    def shift(step, carry):
        r = step // 8
        some = pl.ds(pl.multiple_of(lax.rem(step, 8) * (rows // 8), rows // 8), rows // 8)
        shifted[r, some, :] = pltpu.roll(padded[some, :], r, 1).astype(jnp.bfloat16)
        return carry

    lax.fori_loop(0, ALIGN * 8, shift, 0)
    scale = scale_ref[...]
    fetch.wait()

    for s in range(halves):

        def one_block(i, carry):
            for u in range(2):
                n = i * 2 + u
                start = offsets_ref[s * part + n]
                window = held[pl.ds(lax.div(start, ALIGN), LONG // ALIGN)]
                values = jnp.dot(
                    shifted[lax.rem(start, ALIGN)],
                    window.reshape(LONG, points),
                    preferred_element_type=jnp.float32,
                )
                values = values * scale
                wide[0, n, pl.ds(0, rows), :] = values[:, :128]
                wide[1, n, pl.ds(0, rows), :] = values[:, 128:]
            return carry

        lax.fori_loop(0, part // 2, one_block, 0)
        flat = wide.reshape(2, part * wide.shape[2], 128)

        def place(step, carry):
            for u in range(4):
                i = step * 4 + u
                b_ = u
                c_ = lax.rem(i // 4, 2)
                x_ = lax.rem(i // 8, 4)
                y_ = i // 32
                k = ((y_ * 2 + b_ // 2) * 4 + x_) * 4 + c_ * 2 + b_ % 2
                for h in range(2):
                    for ri in range(2):
                        picked = flat[h, pl.ds(ri * freqs + k, part, stride=wide.shape[2]), :]
                        sent[s, i, h, pl.ds(ri * part, part), :] = picked.astype(jnp.bfloat16)
            return carry

        lax.fori_loop(0, 32, place, 0)
        got[s, mine] = sent[s, mine]
        if s == 0:
            pl.semaphore_wait(barrier, 131)

        for dy in range(4):

            def send(inner, carry):
                b2, y2, x2, c2 = peer(dy, inner)

                @pl.when(jnp.logical_or(inner != 3, dy != 0))
                def _():
                    pltpu.make_async_remote_copy(
                        src_ref=sent.at[s, slot(b2, y2, x2, c2)],
                        dst_ref=got.at[s, mine],
                        send_sem=send_sem.at[s],
                        recv_sem=recv_sem.at[0 if s == 0 else 1 + dy],
                        device_id=device(b2, zh, y2, x2, c2),
                        device_id_type=MESH,
                    ).start()

                return carry

            lax.fori_loop(0, 32, send, 0)

    def arrived(s, lo, count, sem):
        some = got.at[s, pl.ds(lo, count)]
        pltpu.make_async_copy(some, some, sem).wait()

    size = 2 * 4 * blocks
    total[...] = jnp.zeros((size, size), jnp.float32)
    arrived(0, 0, 127, recv_sem.at[0])
    for dy in range(4):
        y_from = lax.rem(y - dy + 4, 4)
        if dy == 0:
            arrived(1, 0, 31, recv_sem.at[1])
        else:
            arrived(1, pl.multiple_of(y_from * 32, 32), 32, recv_sem.at[1 + dy])

        def some_points(step, carry):
            pieces = []
            for u in range(4):
                place_ = y_from * 32 + (step * 4 + u) * 4
                for h in range(2):
                    stack = []
                    for ri in range(2):
                        for b_ in range(4):
                            for s in range(halves):
                                stack.append(got[s, place_ + b_, h, pl.ds(ri * part, part), :])
                    pieces.append(jnp.concatenate(stack, axis=0))
            block = jnp.concatenate(pieces, axis=1)
            total[...] += lax.dot_general(
                block, block, (((1,), (1,)), ((), ())), preferred_element_type=jnp.float32
            )
            return carry

        lax.fori_loop(0, 2, some_points, 0)

    nb = size // 2
    gram_re = total[pl.ds(0, nb), pl.ds(0, nb)] + total[pl.ds(nb, nb), pl.ds(nb, nb)]
    gram_im = total[pl.ds(0, nb), pl.ds(nb, nb)] - total[pl.ds(nb, nb), pl.ds(0, nb)]
    handed[:, 0] = gram_re.reshape(4, blocks, nb)
    handed[:, 1] = gram_im.reshape(4, blocks, nb)

    goal = blk // 2
    here = zh * 2 + lax.rem(blk, 2)
    own = goal == zh

    def hand(b2, carry):
        @pl.when(jnp.logical_or(jnp.logical_not(own), b2 != blk))
        def _():
            pltpu.make_async_remote_copy(
                src_ref=handed.at[b2],
                dst_ref=final.at[here],
                send_sem=hand_sem,
                recv_sem=final_sem,
                device_id=device(b2, goal, y, x, core),
                device_id_type=MESH,
            ).start()

        return carry

    lax.fori_loop(0, 4, hand, 0)

    @pl.when(own)
    def _():
        final[here] = handed[blk]
        three = handed.at[pl.ds(0, 3)]
        pltpu.make_async_copy(three, three, hand_sem).wait()
        three = final.at[pl.ds(0, 3)]
        pltpu.make_async_copy(three, three, final_sem).wait()

    @pl.when(jnp.logical_not(own))
    def _():
        pltpu.make_async_copy(handed, handed, hand_sem).wait()
        pltpu.make_async_copy(final, final, final_sem).wait()

    out_ref[...] = final[pl.ds(0, 2)] + final[pl.ds(2, 2)]
    for s in range(halves):
        some = sent.at[s, pl.ds(0, 127)]
        pltpu.make_async_copy(some, some, send_sem.at[s]).wait()


def on_device(signal, offsets, kept, weights):
    blocks = offsets.shape[0]
    points = signal.shape[1]
    freqs = kept.shape[0]
    groups = lax.axis_size("pts")
    cosine, sine = spectral_table(kept, NFFT)
    scale = jnp.sqrt(weights / (points * groups)).reshape(1, points)
    vmem = pl.BlockSpec(memory_space=pltpu.VMEM)
    part = blocks // 2
    size = 8 * blocks
    return pl.pallas_call(
        fused_kernel,
        out_shape=jax.ShapeDtypeStruct((2, 2, blocks, 4 * blocks), jnp.float32),
        in_specs=[
            pl.BlockSpec(memory_space=pltpu.SMEM),
            vmem,
            vmem,
            vmem,
            pl.BlockSpec(memory_space=pl.ANY),
        ],
        out_specs=vmem,
        scratch_shapes=[
            pltpu.VMEM(((signal.shape[0] + LONG - NFFT) // ALIGN, ALIGN, points), jnp.bfloat16),
            pltpu.VMEM((2 * freqs, LONG), jnp.float32),
            pltpu.VMEM((ALIGN, 2 * freqs, LONG), jnp.bfloat16),
            pltpu.VMEM((2, part, 2 * freqs + PITCH, 128), jnp.float32),
            pltpu.VMEM((2, 128, 2, 2 * part, 128), jnp.bfloat16),
            pltpu.VMEM((2, 128, 2, 2 * part, 128), jnp.bfloat16),
            pltpu.VMEM((size, size), jnp.float32),
            pltpu.VMEM((4, 2, blocks, 4 * blocks), jnp.float32),
            pltpu.VMEM((4, 2, blocks, 4 * blocks), jnp.float32),
            pltpu.SemaphoreType.DMA,
            pltpu.SemaphoreType.DMA((2,)),
            pltpu.SemaphoreType.DMA((5,)),
            pltpu.SemaphoreType.DMA,
            pltpu.SemaphoreType.DMA,
        ],
        compiler_params=pltpu.CompilerParams(collective_id=0, has_side_effects=True),
        name="spod",
    )(offsets, cosine, sine, scale, signal.reshape(-1, ALIGN, points))


def solution(mesh):
    placed = (P("blk", "pts"), P("blk"), P(), P("pts"))
    return jax.shard_map(
        on_device,
        mesh=mesh,
        in_specs=placed,
        out_specs=P("pts", None, "blk", None),
        check_vma=False,
    )
```

time: 573 us -> 140 us (0.24)
  waiting for transfers between devices: 286 us -> 0 us
  Pallas kernels: 0 us -> 134 us
  local copies, waits for them, and re-layouts: 119 us -> 1.47 us
  blocking collectives: 115 us -> 0 us
  matrix products: 32 us -> 0 us
  between operations: 14.2 us -> 0.01 us
    all_gather x1 -> x0, waiting for transfers between devices: 285 us -> none  [on_device(): return gram_terms(moved, lax.all_gather(moved, 'blk', axis=0, tiled=True))]
    pallas_call x0 -> x1, Pallas kernels: none -> 134 us  [on_device(): pl.pallas_call(fused_kernel, out_shape=jax.ShapeDtypeStruct((2, 2, blocks...]
    all_to_all x1 -> x0, blocking collectives: 115 us -> none  [on_device(): lax.all_to_all(spectra, 'pts', split_axis=2, concat_axis=3, tiled=True)]
    gather x96 -> x0, local copies, waits for them, and re-layouts: 99.7 us -> none
    dot_general x5 -> x0, matrix products: 32 us -> none  [the longest x1 12.1 us: on_device(): jnp.einsum('tk,btp->bkp', table, stacked, preferred_element_type=jnp.floa...]
    all_to_all x2 -> x0, local copies, waits for them, and re-layouts: 11.8 us -> none  [on_device(): lax.all_to_all(spectra, 'pts', split_axis=2, concat_axis=3, tiled=True)]
    reshape x1 -> x0, local copies, waits for them, and re-layouts: 6.5 us -> none  [on_device(): spectra = (values * scale[None, None, :]).astype(jnp.bfloat16).reshape(bl...]
  transfers between devices with their start and end apart: 1 -> 0, of which waited for: 1 -> 0; matrix products, arithmetic and copies ran while one was open for 0% -> 0% of each run, Pallas kernels for 0% -> 0%
where the time goes in v2:
time: 140 us
  Pallas kernels  134 us (96%)
  other arithmetic  5.13 us (4%)
  local copies, waits for them, and re-layouts  1.47 us (1%)
    pallas_call x1, Pallas kernels, on_device(): pl.pallas_call(fused_kernel, out_shape=jax.ShapeDtypeStruct((2, 2, blocks...  134 us
    convert_element_type x1, other arithmetic, spectral_table(): return (cosine.astype(jnp.bfloat16), sine.astype(jnp.bfloat16))  3.89 us

profile of v2, /device:TPU:1, one launch (start us, length us, event | category | flops | bytes accessed | tf_op | source)
XLA Modules:
  0.0 140.2 jit_solution(2223682174020989591)
XLA Ops:
  0.0 1.2 multiply_sqrt_fusion
  1.3 3.9 %multiply_convert_fusion = (bf16[128,1024]{1,0:T(8,128)(2,1)}, bf16[128,1024]{1,0:T(8,128)(2,1)}) fusion(f32[1024]{0:T(1024)} %constant.27, s32[128]{0:T(128)} %param.8, f32[1024]{0:T(1024)} %constant.26), kind=kLoop, calls=%fused_computation.6 | loop fusion | flops 2359296 | bytes 532992 | tf_op jit(solution)/shard_map/convert_element_type | solution.py:30
  5.1 133.6 %spod.1 = f32[2,2,32,128]{3,2,1,0:T(8,128)} custom-call(s32[32]{0:T(128)} %offsets_ref.1, bf16[128,1024]{1,0:T(8,128)(2,1)} %get-tuple-element.6.cos_ref, bf16[128,1024]{1,0:T(8,128)(2,1)} %get-tuple-element.5.sin_ref, f32[1,256]{1,0:T(1,128)} %bitcast.3, bf16[1056,16,256]{2,1,0:T(8,128)(2,1)} %bitcast.2), custom_call_target="tpu_custom_call" | custom-call | tf_op jit(solution)/shard_map/spod/pallas_call | solution.py:258
  138.7 1.5 %copy.8 = f32[2,2,32,128]{3,2,1,0:T(8,128)} copy(f32[2,2,32,128]{3,2,1,0:T(8,128)} %spod.1) | data formatting | bytes 131072
